TPU v7x, 32 devices: a whole 2x2x4 slice. The times are simulated.
32 devices in a mesh: grp: 4 (over z), ctx: 2 (over y), wid: 4 (over x, core).
Axes of the slice: x: 2, y: 2, z: 4, core: 2. Of those that a mesh axis runs over, the one named last changes fastest.
Arguments:
- query: bfloat16 [256, 64, 128], P(None, 'wid'), may hold values from -64 to 64
- keys: bfloat16 [4, 512, 8, 128], P(None, ('grp', 'ctx'), 'wid'), may hold values from -64 to 64
- values: bfloat16 [4, 512, 8, 128], P(None, ('grp', 'ctx'), 'wid'), may hold values from -6 to 6
- lengths: int32 [4, 8], replicated, may hold values from 32 to 64
- query_pos: int32 [256], replicated, may hold values from 128 to 511
- resid: bfloat16 [256, 5120], P('wid', ('grp', 'ctx')), may hold values from -1.1953125 to 1.1953125
- out_weight: bfloat16 [8192, 5120], P('wid', ('grp', 'ctx')), may hold values from -0.0625 to 0.0625
- enc_weight: bfloat16 [5120, 24576], P('wid', ('grp', 'ctx')), may hold values from -0.078125 to 0.078125
- enc_bias: float32 [24576], P(('grp', 'ctx')), may hold values from -3 to 3
- dec_weight: bfloat16 [24576, 5120], P(('grp', 'ctx'), 'wid'), may hold values from -0.078125 to 0.078125
- dec_bias: float32 [5120], P('wid'), may hold values from -3 to 3
Outputs:
- layer_out: bfloat16 [256, 5120], P('wid', ('grp', 'ctx'))
- enc_grad: bfloat16 [5120, 24576], P('wid', ('grp', 'ctx'))
- enc_bias_grad: float32 [24576], P(('grp', 'ctx'))
- dec_grad: bfloat16 [24576, 5120], P(('grp', 'ctx'), 'wid')
- dec_bias_grad: float32 [5120], P('wid')
Inputs may be any that keep to these rules, and one draw needn't show every extreme that they name: `lengths`: live slots of a shard are its first ones.
All inputs are finite; a program needn't handle non-finite values.
Results may differ from a plain program's by a relative error of at most 0.024.
Values may be sent and summed in bfloat16 or wider, within the bound.
A program may use at most 128 MiB of HBM per device.

v0:
```python
import jax
import jax.numpy as jnp
from jax import lax
from jax.sharding import PartitionSpec as P

HD = 128


def body(
    query,
    keys,
    values,
    lengths,
    query_pos,
    resid,
    out_weight,
    enc_weight,
    enc_bias,
    dec_weight,
    dec_bias,
):
    seq_count, slot_count, kv_local, head_dim = keys.shape
    row_count = query.shape[0]
    heads_local = query.shape[1]
    group_size = heads_local // kv_local
    rows_each = row_count // seq_count
    shard_pos = lax.axis_index(("grp", "ctx"))
    shard_ids = jnp.arange(lengths.shape[1], dtype=jnp.int32)
    offset = jnp.sum(jnp.where(shard_ids[None, :] < shard_pos, lengths, 0), axis=1)
    live_count = jnp.sum(jnp.where(shard_ids[None, :] == shard_pos, lengths, 0), axis=1)
    slot_ids = jnp.arange(slot_count, dtype=jnp.int32)
    key_pos = offset[:, None] + slot_ids[None, :]
    live_slot = slot_ids[None, :] < live_count[:, None]
    row_position = query_pos.reshape(seq_count, rows_each)
    visible = live_slot[:, None, :] & (key_pos[:, None, :] <= row_position[:, :, None])
    visible_mask = visible[:, :, None, None, :]
    q_view = query.reshape(seq_count, rows_each, kv_local, group_size, head_dim)
    scores = jnp.einsum(
        "srkgd,sjkd->srkgj", q_view, keys, preferred_element_type=jnp.float32
    ) * HD ** (-0.5)
    local_peak = jnp.max(jnp.where(visible_mask, scores, -1e30), axis=-1)
    peak = lax.pmax(local_peak, ("grp", "ctx"))
    weights = jnp.where(visible_mask, jnp.exp(scores - peak[..., None]), 0.0)
    weight_sum = jnp.sum(weights, axis=-1)
    weights_low = weights.astype(jnp.bfloat16)
    weighted = jnp.einsum(
        "srkgj,sjkd->srkgd", weights_low, values, preferred_element_type=jnp.float32
    )
    weight_sum, weighted = (weight_sum, weighted)
    weight_sum, weighted = lax.psum((weight_sum, weighted), ("grp", "ctx"))
    attention = (weighted / weight_sum[..., None]).astype(jnp.bfloat16)
    attention = attention.reshape(row_count, heads_local * head_dim)
    projected = jnp.dot(attention, out_weight, preferred_element_type=jnp.float32)
    mixed = lax.psum_scatter(
        projected.astype(jnp.bfloat16), "wid", scatter_dimension=0, tiled=True
    ).astype(jnp.float32)
    layer_out = (mixed + resid.astype(jnp.float32)).astype(jnp.bfloat16)
    wide_rows = lax.all_gather(layer_out, ("grp", "ctx"), axis=1, tiled=True)
    block = lax.all_to_all(wide_rows, "wid", split_axis=1, concat_axis=0, tiled=True)
    enc_part = jnp.dot(block, enc_weight, preferred_element_type=jnp.float32)
    preact = lax.psum(enc_part.astype(jnp.bfloat16), "wid").astype(jnp.float32) + enc_bias
    latents = (jax.nn.softplus(4.0 * preact) * 0.25).astype(jnp.bfloat16)
    row_scale = row_count ** (-0.5)
    recon = lax.psum_scatter(
        jnp.dot(latents, dec_weight, preferred_element_type=jnp.float32),
        ("grp", "ctx"),
        scatter_dimension=0,
        tiled=True,
    )
    piece_len = recon.shape[0]
    target = lax.dynamic_slice_in_dim(block, shard_pos * piece_len, piece_len, 0).astype(
        jnp.float32
    )
    scaled_error = ((recon + dec_bias - target) * row_scale).astype(jnp.bfloat16)
    error_all = lax.all_gather(scaled_error, ("grp", "ctx"), axis=0, tiled=True)
    dec_bias_grad = jnp.sum(error_all, axis=0, dtype=jnp.float32)
    latent_part = lax.dot_general(
        error_all, dec_weight, (((1,), (1,)), ((), ())), preferred_element_type=jnp.float32
    )
    dec_grad = lax.dot_general(
        latents, error_all, (((0,), (0,)), ((), ())), preferred_element_type=jnp.float32
    )
    latent_grad = lax.psum(latent_part.astype(jnp.bfloat16), "wid").astype(jnp.float32)
    preact_grad = (latent_grad * jax.nn.sigmoid(4.0 * preact)).astype(jnp.bfloat16)
    enc_grad = lax.dot_general(
        block, preact_grad, (((0,), (0,)), ((), ())), preferred_element_type=jnp.float32
    ).astype(jnp.bfloat16)
    enc_bias_grad = jnp.sum(preact_grad, axis=0, dtype=jnp.float32)
    return (layer_out, enc_grad, enc_bias_grad, dec_grad.astype(jnp.bfloat16), dec_bias_grad)


def solution(mesh):
    placed = (
        P(None, "wid", None),
        P(None, ("grp", "ctx"), "wid", None),
        P(None, ("grp", "ctx"), "wid", None),
        P(),
        P(),
        P("wid", ("grp", "ctx")),
        P("wid", ("grp", "ctx")),
        P("wid", ("grp", "ctx")),
        P(("grp", "ctx")),
        P(("grp", "ctx"), "wid"),
        P("wid"),
    )
    return jax.shard_map(
        body,
        mesh=mesh,
        in_specs=placed,
        out_specs=(
            P("wid", ("grp", "ctx")),
            P("wid", ("grp", "ctx")),
            P(("grp", "ctx")),
            P(("grp", "ctx"), "wid"),
            P("wid"),
        ),
        check_vma=False,
    )
```

profile of v0, /device:TPU:0, one launch (start us, length us, event | category | flops | bytes accessed | tf_op | source)
XLA Modules:
  0.0 456.0 jit_solution(1669517848478432027)
XLA Ops:
  7.2 0.0 copy-start
  7.2 0.0 all-reduce.4.cloned.1.call-start
  7.2 0.9 le.20
  8.1 0.8 select_reduce_fusion.1
  9.0 0.1 iota_add_fusion
  9.0 0.1 iota_compare_fusion
  9.1 0.1 compare_and_fusion
  9.3 3.8 fusion.2
  13.0 39.0 %pmax.7 = f32[4,64,2,8]{1,3,2,0:T(8,128)S(1)} all-reduce(f32[4,64,2,8]{1,3,2,0:T(8,128)S(1)} %get-tuple-element.11), channel_id=1, replica_groups=mesh['grp'=4,'ctx'=2,'wid'=4] {'grp','ctx'}, use_global_device_ids=true, to_apply=%region_3.4 | all-reduce | flops 4096 | bytes 32768 | tf_op jit(solution)/shard_map/pmax | solution.py:42
  52.0 3.2 fusion.5
  55.3 2.4 copy.29
  57.7 3.0 convolution_bitcast_fusion
  60.6 0.0 all-reduce.4.cloned.1.call-update
  60.7 0.0 reduce-scatter.3.cloned.1.call-start
  60.7 34.2 %psum.29 = f32[4,64,2,8]{1,3,2,0:T(8,128)S(1)} all-reduce(f32[4,64,2,8]{1,3,2,0:T(8,128)S(1)} %get-tuple-element.9), channel_id=1, replica_groups=mesh['grp'=4,'ctx'=2,'wid'=4] {'grp','ctx'}, use_global_device_ids=true, to_apply=%region_6.7 | all-reduce | flops 4096 | bytes 32768 | tf_op jit(solution)/shard_map/psum | solution.py:50
  94.9 0.1 copy.31
  95.0 65.7 %all-reduce.4.cloned.1.call-done = f32[4,64,2,8,128]{4,3,1,2,0:T(8,128)} async-done(((f32[4,64,2,8,128]{4,3,1,2,0:T(8,128)}), f32[4,64,2,8,128]{4,3,1,2,0:T(8,128)}) %all-reduce.4.cloned.1.call-update) | async-done | bytes 2097168 | tf_op jit(solution)/shard_map/psum | solution.py:50
  160.8 1.9 divide_convert_fusion
  162.7 1.2 copy.32
  163.9 2.3 reshape.71
  166.2 2.9 convolution_convert_fusion.4
  169.1 0.0 reduce-scatter.3.cloned.1.call-update
  169.1 0.0 all-reduce.6.cloned.1.call-start
  169.2 19.8 %reduce-scatter.3.cloned.1.call-done = bf16[64,640]{1,0:T(8,128)(2,1)} async-done(((bf16[256,640]{1,0:T(8,128)(2,1)}), bf16[64,640]{1,0:T(8,128)(2,1)}) %reduce-scatter.3.cloned.1.call-update) | async-done | bytes 81936 | tf_op jit(solution)/shard_map/reduce_scatter | solution.py:54
  189.0 0.9 add_convert_fusion
  189.9 0.0 copy-start.2
  189.9 32.1 %all_gather.6 = bf16[64,5120]{1,0:T(8,128)(2,1)S(1)} all-gather(bf16[64,640]{1,0:T(8,128)(2,1)S(1)} %add_convert_fusion), channel_id=1, replica_groups=mesh['grp'=4,'ctx'=2,'wid'=4] {'grp','ctx'}, dimensions={1}, use_global_device_ids=true | all-gather | bytes 737280 | tf_op jit(solution)/shard_map/all_gather | solution.py:58
  222.1 12.6 %all_to_all.19 = bf16[64,4,1280]{2,0,1:T(8,128)(2,1)S(1)} all-to-all(bf16[64,4,1280]{2,0,1:T(8,128)(2,1)S(1)} %bitcast.41), channel_id=1, replica_groups=mesh['grp'=4,'ctx'=2,'wid'=4] {'wid'}, dimensions={1} | all-to-all | bytes 1310720 | tf_op jit(solution)/shard_map/all_to_all | solution.py:59
  234.7 6.6 %convolution_convert_fusion.3 = bf16[256,3072]{1,0:T(8,128)(2,1)} fusion(bf16[256,1280]{1,0:T(8,128)(2,1)S(1)} %bitcast.38, bf16[1280,3072]{1,0:T(8,128)(2,1)} %param.18), kind=kOutput, calls=%fused_computation.4 | convolution fusion | flops 2014052352 | bytes 10092544 | tf_op jit(solution)/shard_map/dot_general | solution.py:60
  241.3 0.0 all-reduce.6.cloned.1.call-update
  241.4 0.0 copy-start.6
  241.4 0.0 reduce-scatter.5.cloned.1.call-start
  241.4 42.7 %all-reduce.6.cloned.1.call-done = bf16[256,3072]{1,0:T(8,128)(2,1)} async-done(((bf16[256,3072]{1,0:T(8,128)(2,1)}), bf16[256,3072]{1,0:T(8,128)(2,1)}) %all-reduce.6.cloned.1.call-update) | async-done | bytes 1572880 | tf_op jit(solution)/shard_map/psum | solution.py:61
  284.1 8.8 %fusion.12 = f32[256,1280]{1,0:T(8,128)} fusion(bf16[3072,1280]{1,0:T(8,128)(2,1)} %param.20, bf16[256,3072]{1,0:T(8,128)(2,1)} %all-reduce.6.cloned.1.call-done, f32[3072]{0:T(1024)S(1)} %copy-done.5), kind=kOutput, calls=%fused_computation.35 | convolution fusion | flops 2021916672 | bytes 10760192 | tf_op jit(solution)/shard_map/dot_general | solution.py:65
  292.9 0.0 reduce-scatter.5.cloned.1.call-update
  293.0 0.0 all-reduce.8.cloned.1.call-start
  293.0 65.3 %reduce-scatter.5.cloned.1.call-done = f32[32,1280]{1,0:T(8,128)} async-done(((f32[256,1280]{1,0:T(8,128)}), f32[32,1280]{1,0:T(8,128)}) %reduce-scatter.5.cloned.1.call-update) | async-done | bytes 163856 | tf_op jit(solution)/shard_map/reduce_scatter | solution.py:64
  358.3 0.0 copy-done.6
  358.3 0.9 multiply_convert_fusion.1
  359.2 32.1 %all_gather.7 = bf16[256,1280]{1,0:T(8,128)(2,1)S(1)} all-gather(bf16[32,1280]{1,0:T(8,128)(2,1)S(1)} %multiply_convert_fusion.1), channel_id=1, replica_groups=mesh['grp'=4,'ctx'=2,'wid'=4] {'grp','ctx'}, dimensions={0}, use_global_device_ids=true | all-gather | bytes 737280 | tf_op jit(solution)/shard_map/all_gather | solution.py:75
  391.4 0.8 copy-done.1
  392.2 6.6 %convolution_convert_fusion.2 = bf16[256,3072]{1,0:T(8,128)(2,1)} fusion(bf16[256,1280]{1,0:T(8,128)(2,1)S(1)} %all_gather.7, bf16[3072,1280]{1,0:T(8,128)(2,1)} %param.20), kind=kOutput, calls=%fused_computation.3 | convolution fusion | flops 2014052352 | bytes 10092544 | tf_op jit(solution)/shard_map/dot_general | solution.py:77
  398.8 0.0 all-reduce.8.cloned.1.call-update
  398.8 1.8 convert_reduce_fusion.1
  400.6 9.0 %convolution_convert_fusion = bf16[3072,1280]{1,0:T(8,128)(2,1)} fusion(bf16[256,1280]{1,0:T(8,128)(2,1)} %copy-done.1, bf16[256,3072]{1,0:T(8,128)(2,1)} %all-reduce.6.cloned.1.call-done, f32[3072]{0:T(1024)S(1)} %copy-done.5), kind=kOutput, calls=%fused_computation | convolution fusion | flops 2025848832 | bytes 10104832 | tf_op jit(solution)/shard_map/dot_general | solution.py:80
  409.6 30.8 %all-reduce.8.cloned.1.call-done = bf16[256,3072]{1,0:T(8,128)(2,1)} async-done(((bf16[256,3072]{1,0:T(8,128)(2,1)}), bf16[256,3072]{1,0:T(8,128)(2,1)}) %all-reduce.8.cloned.1.call-update) | async-done | bytes 1572880 | tf_op jit(solution)/shard_map/psum | solution.py:83
  440.4 3.6 convert_reduce_fusion
  444.0 5.5 %convolution_convert_fusion.1 = bf16[1280,3072]{1,0:T(8,128)(2,1)} fusion(bf16[256,1280]{1,0:T(8,128)(2,1)S(1)} %bitcast.40, bf16[256,3072]{1,0:T(8,128)(2,1)S(1)} %get-tuple-element.8), kind=kOutput, calls=%fused_computation.1 | convolution fusion | flops 2017198080 | bytes 10092544 | tf_op jit(solution)/shard_map/dot_general | solution.py:85
  (11 shorter events, 0.1 us)
Async XLA Ops:
  7.2 159.0 %copy-start = (bf16[2048,640]{1,0:T(8,128)(2,1)S(1)}, bf16[2048,640]{1,0:T(8,128)(2,1)}, u32[]{:S(2)}) copy-start(bf16[2048,640]{1,0:T(8,128)(2,1)} %param.17) | copy-start | bytes 7864324
  7.2 153.6 %all-reduce.4.cloned.1.call-start = ((), (), s32[]{:S(2)}) async-start(), calls=%async_computation.3 | async-start | bytes 4194304 | tf_op jit(solution)/shard_map/psum | solution.py:50
  13.0 44.6 %copy-start.3 = (bf16[4,64,2,128]{3,2,1,0:T(2,128)(2,1)S(1)}, bf16[4,64,2,128]{3,2,1,0:T(2,128)(2,1)}, u32[]{:S(2)}) copy-start(bf16[4,64,2,128]{3,2,1,0:T(2,128)(2,1)} %param.13) | copy-start | bytes 393220
  60.7 128.4 %reduce-scatter.3.cloned.1.call-start = ((), (), s32[]{:S(2)}) async-start(), calls=%async_computation.4 | async-start | bytes 409600 | tf_op jit(solution)/shard_map/reduce_scatter | solution.py:54
  163.9 25.1 %copy-start.4 = (bf16[64,640]{1,0:T(8,128)(2,1)S(1)}, bf16[64,640]{1,0:T(8,128)(2,1)}, u32[]{:S(2)}) copy-start(bf16[64,640]{1,0:T(8,128)(2,1)} %param.16) | copy-start | bytes 245764
  169.1 114.9 %all-reduce.6.cloned.1.call-start = ((), (), s32[]{:S(2)}) async-start(), calls=%async_computation.5 | async-start | bytes 3145728 | tf_op jit(solution)/shard_map/psum | solution.py:61
  189.9 51.4 %copy-start.2 = (bf16[64,640]{1,0:T(8,128)(2,1)}, bf16[64,640]{1,0:T(8,128)(2,1)S(1)}, u32[]{:S(2)}) copy-start(bf16[64,640]{1,0:T(8,128)(2,1)S(1)} %add_convert_fusion) | copy-start | bytes 245764
  234.7 49.3 %copy-start.5 = (f32[3072]{0:T(1024)S(1)}, f32[3072]{0:T(1024)}, u32[]{:S(2)}) copy-start(f32[3072]{0:T(1024)} %param.19) | copy-start | bytes 36868
  241.4 116.9 %copy-start.6 = (f32[1280]{0:T(1024)S(1)}, f32[1280]{0:T(1024)}, u32[]{:S(2)}) copy-start(f32[1280]{0:T(1024)} %param.21) | copy-start | bytes 15364
  241.4 116.9 %reduce-scatter.5.cloned.1.call-start = ((), (), s32[]{:S(2)}) async-start(), calls=%async_computation.6 | async-start | bytes 1474560 | tf_op jit(solution)/shard_map/reduce_scatter | solution.py:64
  293.0 147.5 %all-reduce.8.cloned.1.call-start = ((), (), s32[]{:S(2)}) async-start(), calls=%async_computation.7 | async-start | bytes 3145728 | tf_op jit(solution)/shard_map/psum | solution.py:83
  391.4 0.8 copy-start.1
Sparse Core Ops, SparseCore 0:
  60.8 99.9 all-reduce.3
  169.3 19.6 reduce-scatter.2
  241.5 42.5 all-reduce.5
  293.1 65.1 reduce-scatter.4
  398.9 41.4 all-reduce.7
where the time goes:
time: 457 us; the launch traced here: 456 us
  waiting for transfers between devices  224 us (49%)
  blocking collectives  150 us (33%)
  matrix products  46.2 us (10%)
  between operations  13.9 us (3%)
  other arithmetic  13.5 us (3%)
  local copies, waits for them, and re-layouts  7.82 us (2%)
    psum x1, waiting for transfers between devices, body(): weight_sum, weighted = lax.psum((weight_sum, weighted), ('grp', 'ctx'))  65.7 us
    reduce_scatter x1, waiting for transfers between devices, body(): lax.psum_scatter(jnp.dot(latents, dec_weight, preferred_element_type=jnp....  65.3 us
    psum x1, waiting for transfers between devices, body(): lax.psum(enc_part.astype(jnp.bfloat16), 'wid').astype(jnp.float32)  42.7 us
    pmax x1, blocking collectives, body(): peak = lax.pmax(local_peak, ('grp', 'ctx'))  39 us
    psum x1, blocking collectives, body(): weight_sum, weighted = lax.psum((weight_sum, weighted), ('grp', 'ctx'))  34.2 us
    all_gather x1, blocking collectives, body(): wide_rows = lax.all_gather(layer_out, ('grp', 'ctx'), axis=1, tiled=True)  32.1 us
    all_gather x1, blocking collectives, body(): error_all = lax.all_gather(scaled_error, ('grp', 'ctx'), axis=0, tiled=True)  32.1 us
    psum x1, waiting for transfers between devices, body(): lax.psum(latent_part.astype(jnp.bfloat16), 'wid').astype(jnp.float32)  30.8 us
  transfers between devices with their start and end apart: 5, of which 5 were waited for; matrix products, arithmetic and copies ran while one was open for 2% of the time, Pallas kernels for 0%

commit v1 on v0

--- a/solution.py
+++ b/solution.py
@@ -4,6 +4,11 @@
 from jax.sharding import PartitionSpec as P
 
 HD = 128
+
+
+def one_after_other(x, one, other):
+    inner = lax.psum(x, one)
+    return lax.psum(inner, other)
 
 
 def body(
@@ -47,7 +52,7 @@
         "srkgj,sjkd->srkgd", weights_low, values, preferred_element_type=jnp.float32
     )
     weight_sum, weighted = (weight_sum, weighted)
-    weight_sum, weighted = lax.psum((weight_sum, weighted), ("grp", "ctx"))
+    weight_sum, weighted = one_after_other((weight_sum, weighted), "ctx", "grp")
     attention = (weighted / weight_sum[..., None]).astype(jnp.bfloat16)
     attention = attention.reshape(row_count, heads_local * head_dim)
     projected = jnp.dot(attention, out_weight, preferred_element_type=jnp.float32)

time: 457 us -> 506 us (1.11)
  waiting for transfers between devices: 224 us -> 280 us
  blocking collectives: 150 us -> 144 us
    psum x1 -> x2, waiting for transfers between devices: 65.7 us -> 122 us  [the longest x1 61.2 us: one_after_other(): return lax.psum(inner, other)]
    psum x1 -> x2, blocking collectives: 34.2 us -> 28.1 us  [the longest x1 20.9 us: one_after_other(): return lax.psum(inner, other)]
  transfers between devices with their start and end apart: 5 -> 6, of which waited for: 5 -> 6; matrix products, arithmetic and copies ran while one was open for 2% -> 2% of each run, Pallas kernels for 0% -> 0%
where the time goes in v1:
time: 506 us
  waiting for transfers between devices  280 us (55%)
  blocking collectives  144 us (28%)
  matrix products  46.2 us (9%)
  between operations  14.2 us (3%)
  other arithmetic  13.5 us (3%)
  local copies, waits for them, and re-layouts  7.82 us (2%)
    reduce_scatter x1, waiting for transfers between devices, body(): lax.psum_scatter(jnp.dot(latents, dec_weight, preferred_element_type=jnp....  65.3 us
    psum x1, waiting for transfers between devices, one_after_other(): return lax.psum(inner, other)  61.2 us
    psum x1, waiting for transfers between devices, one_after_other(): inner = lax.psum(x, one)  60.3 us
    psum x1, waiting for transfers between devices, body(): lax.psum(enc_part.astype(jnp.bfloat16), 'wid').astype(jnp.float32)  42.8 us
    pmax x1, blocking collectives, body(): peak = lax.pmax(local_peak, ('grp', 'ctx'))  39 us
    all_gather x1, blocking collectives, body(): error_all = lax.all_gather(scaled_error, ('grp', 'ctx'), axis=0, tiled=True)  32.1 us
    all_gather x1, blocking collectives, body(): wide_rows = lax.all_gather(layer_out, ('grp', 'ctx'), axis=1, tiled=True)  31.9 us
    psum x1, waiting for transfers between devices, body(): lax.psum(latent_part.astype(jnp.bfloat16), 'wid').astype(jnp.float32)  30.8 us
  transfers between devices with their start and end apart: 6, of which 6 were waited for; matrix products, arithmetic and copies ran while one was open for 2% of the time, Pallas kernels for 0%

profile of v1, /device:TPU:0, one launch (start us, length us, event | category | flops | bytes accessed | tf_op | source)
XLA Modules:
  0.0 505.8 jit_solution(15836870261231741317)
XLA Ops:
  7.2 0.0 all-reduce.5.cloned.1.call-start
  7.2 0.9 le.20
  8.1 0.8 select_reduce_fusion.1
  9.0 0.1 iota_add_fusion
  9.0 0.1 iota_compare_fusion
  9.1 0.1 compare_and_fusion
  9.3 3.8 fusion.2
  13.0 39.0 %pmax.7 = f32[4,64,2,8]{1,3,2,0:T(8,128)S(1)} all-reduce(f32[4,64,2,8]{1,3,2,0:T(8,128)S(1)} %get-tuple-element.11), channel_id=1, replica_groups=mesh['grp'=4,'ctx'=2,'wid'=4] {'grp','ctx'}, use_global_device_ids=true, to_apply=%region_3.4 | all-reduce | flops 4096 | bytes 32768 | tf_op jit(solution)/shard_map/pmax | solution.py:47
  52.0 3.2 fusion.5
  55.3 2.4 copy.29
  57.7 3.0 convolution_bitcast_fusion
  60.6 0.0 all-reduce.5.cloned.1.call-update
  60.7 0.0 all-reduce.7.cloned.1.call-start
  60.7 60.3 %all-reduce.5.cloned.1.call-done = f32[4,64,2,8,128]{4,3,1,2,0:T(8,128)} async-done(((f32[4,64,2,8,128]{4,3,1,2,0:T(8,128)}), f32[4,64,2,8,128]{4,3,1,2,0:T(8,128)}) %all-reduce.5.cloned.1.call-update) | async-done | bytes 2097168 | tf_op jit(solution)/shard_map/psum | solution.py:10
  121.0 0.0 all-reduce.7.cloned.1.call-update
  121.1 0.0 reduce-scatter.3.cloned.1.call-start
  121.1 7.2 %psum.44 = f32[4,64,2,8]{1,3,2,0:T(8,128)S(1)} all-reduce(f32[4,64,2,8]{1,3,2,0:T(8,128)S(1)} %get-tuple-element.9), channel_id=1, replica_groups=mesh['grp'=4,'ctx'=2,'wid'=4] {'ctx'}, use_global_device_ids=true, to_apply=%region_7.8 | all-reduce | flops 4096 | bytes 32768 | tf_op jit(solution)/shard_map/psum | solution.py:10
  128.3 20.9 %psum.45 = f32[4,64,2,8]{1,3,2,0:T(8,128)S(1)} all-reduce(f32[4,64,2,8]{1,3,2,0:T(8,128)S(1)} %psum.44), channel_id=1, replica_groups=mesh['grp'=4,'ctx'=2,'wid'=4] {'grp'}, use_global_device_ids=true, to_apply=%region_8.9 | all-reduce | flops 4096 | bytes 32768 | tf_op jit(solution)/shard_map/psum | solution.py:11
  149.2 0.1 copy.31
  149.4 61.2 %all-reduce.7.cloned.1.call-done = f32[4,64,2,8,128]{4,3,1,2,0:T(8,128)} async-done(((f32[4,64,2,8,128]{4,3,1,2,0:T(8,128)}), f32[4,64,2,8,128]{4,3,1,2,0:T(8,128)}) %all-reduce.7.cloned.1.call-update) | async-done | bytes 2097168 | tf_op jit(solution)/shard_map/psum | solution.py:11
  210.6 1.9 divide_convert_fusion
  212.5 1.2 copy.32
  213.7 2.3 reshape.71
  216.0 2.9 convolution_convert_fusion.4
  218.9 0.0 reduce-scatter.3.cloned.1.call-update
  218.9 0.0 all-reduce.9.cloned.1.call-start
  219.0 19.6 %reduce-scatter.3.cloned.1.call-done = bf16[64,640]{1,0:T(8,128)(2,1)} async-done(((bf16[256,640]{1,0:T(8,128)(2,1)}), bf16[64,640]{1,0:T(8,128)(2,1)}) %reduce-scatter.3.cloned.1.call-update) | async-done | bytes 81936 | tf_op jit(solution)/shard_map/reduce_scatter | solution.py:59
  238.5 0.9 add_convert_fusion
  239.5 31.9 %all_gather.6 = bf16[64,5120]{1,0:T(8,128)(2,1)S(1)} all-gather(bf16[64,640]{1,0:T(8,128)(2,1)S(1)} %add_convert_fusion), channel_id=1, replica_groups=mesh['grp'=4,'ctx'=2,'wid'=4] {'grp','ctx'}, dimensions={1}, use_global_device_ids=true | all-gather | bytes 737280 | tf_op jit(solution)/shard_map/all_gather | solution.py:63
  271.4 12.6 %all_to_all.19 = bf16[64,4,1280]{2,0,1:T(8,128)(2,1)S(1)} all-to-all(bf16[64,4,1280]{2,0,1:T(8,128)(2,1)S(1)} %bitcast.41), channel_id=1, replica_groups=mesh['grp'=4,'ctx'=2,'wid'=4] {'wid'}, dimensions={1} | all-to-all | bytes 1310720 | tf_op jit(solution)/shard_map/all_to_all | solution.py:64
  284.1 6.6 %convolution_convert_fusion.3 = bf16[256,3072]{1,0:T(8,128)(2,1)} fusion(bf16[256,1280]{1,0:T(8,128)(2,1)S(1)} %bitcast.38, bf16[1280,3072]{1,0:T(8,128)(2,1)} %param.18), kind=kOutput, calls=%fused_computation.4 | convolution fusion | flops 2014052352 | bytes 10092544 | tf_op jit(solution)/shard_map/dot_general | solution.py:65
  290.6 0.0 all-reduce.9.cloned.1.call-update
  290.7 0.0 reduce-scatter.5.cloned.1.call-start
  290.7 42.8 %all-reduce.9.cloned.1.call-done = bf16[256,3072]{1,0:T(8,128)(2,1)} async-done(((bf16[256,3072]{1,0:T(8,128)(2,1)}), bf16[256,3072]{1,0:T(8,128)(2,1)}) %all-reduce.9.cloned.1.call-update) | async-done | bytes 1572880 | tf_op jit(solution)/shard_map/psum | solution.py:66
  333.6 8.8 %fusion.12 = f32[256,1280]{1,0:T(8,128)} fusion(bf16[3072,1280]{1,0:T(8,128)(2,1)} %param.20, bf16[256,3072]{1,0:T(8,128)(2,1)} %all-reduce.9.cloned.1.call-done, f32[3072]{0:T(1024)S(1)} %copy-done.5), kind=kOutput, calls=%fused_computation.35 | convolution fusion | flops 2021916672 | bytes 10760192 | tf_op jit(solution)/shard_map/dot_general | solution.py:70
  342.4 0.0 reduce-scatter.5.cloned.1.call-update
  342.4 0.0 all-reduce.11.cloned.1.call-start
  342.5 65.3 %reduce-scatter.5.cloned.1.call-done = f32[32,1280]{1,0:T(8,128)} async-done(((f32[256,1280]{1,0:T(8,128)}), f32[32,1280]{1,0:T(8,128)}) %reduce-scatter.5.cloned.1.call-update) | async-done | bytes 163856 | tf_op jit(solution)/shard_map/reduce_scatter | solution.py:69
  407.8 0.9 multiply_convert_fusion.1
  408.7 32.1 %all_gather.7 = bf16[256,1280]{1,0:T(8,128)(2,1)S(1)} all-gather(bf16[32,1280]{1,0:T(8,128)(2,1)S(1)} %multiply_convert_fusion.1), channel_id=1, replica_groups=mesh['grp'=4,'ctx'=2,'wid'=4] {'grp','ctx'}, dimensions={0}, use_global_device_ids=true | all-gather | bytes 737280 | tf_op jit(solution)/shard_map/all_gather | solution.py:80
  440.8 0.8 copy-done.1
  441.7 6.6 %convolution_convert_fusion.2 = bf16[256,3072]{1,0:T(8,128)(2,1)} fusion(bf16[256,1280]{1,0:T(8,128)(2,1)S(1)} %all_gather.7, bf16[3072,1280]{1,0:T(8,128)(2,1)} %param.20), kind=kOutput, calls=%fused_computation.3 | convolution fusion | flops 2014052352 | bytes 10092544 | tf_op jit(solution)/shard_map/dot_general | solution.py:82
  448.3 0.0 all-reduce.11.cloned.1.call-update
  448.3 1.8 convert_reduce_fusion.1
  450.1 9.0 %convolution_convert_fusion = bf16[3072,1280]{1,0:T(8,128)(2,1)} fusion(bf16[256,1280]{1,0:T(8,128)(2,1)} %copy-done.1, bf16[256,3072]{1,0:T(8,128)(2,1)} %all-reduce.9.cloned.1.call-done, f32[3072]{0:T(1024)S(1)} %copy-done.5), kind=kOutput, calls=%fused_computation | convolution fusion | flops 2025848832 | bytes 10104832 | tf_op jit(solution)/shard_map/dot_general | solution.py:85
  459.1 30.8 %all-reduce.11.cloned.1.call-done = bf16[256,3072]{1,0:T(8,128)(2,1)} async-done(((bf16[256,3072]{1,0:T(8,128)(2,1)}), bf16[256,3072]{1,0:T(8,128)(2,1)}) %all-reduce.11.cloned.1.call-update) | async-done | bytes 1572880 | tf_op jit(solution)/shard_map/psum | solution.py:88
  489.9 3.6 convert_reduce_fusion
  493.5 5.5 %convolution_convert_fusion.1 = bf16[1280,3072]{1,0:T(8,128)(2,1)} fusion(bf16[256,1280]{1,0:T(8,128)(2,1)S(1)} %bitcast.40, bf16[256,3072]{1,0:T(8,128)(2,1)S(1)} %get-tuple-element.8), kind=kOutput, calls=%fused_computation.1 | convolution fusion | flops 2017198080 | bytes 10092544 | tf_op jit(solution)/shard_map/dot_general | solution.py:90
  (15 shorter events, 0.1 us)
Async XLA Ops:
  7.2 208.8 %copy-start = (bf16[2048,640]{1,0:T(8,128)(2,1)S(1)}, bf16[2048,640]{1,0:T(8,128)(2,1)}, u32[]{:S(2)}) copy-start(bf16[2048,640]{1,0:T(8,128)(2,1)} %param.17) | copy-start | bytes 7864324
  7.2 113.9 %all-reduce.5.cloned.1.call-start = ((), (), s32[]{:S(2)}) async-start(), calls=%async_computation.3 | async-start | bytes 4194304 | tf_op jit(solution)/shard_map/psum | solution.py:10
  13.0 44.6 %copy-start.3 = (bf16[4,64,2,128]{3,2,1,0:T(2,128)(2,1)S(1)}, bf16[4,64,2,128]{3,2,1,0:T(2,128)(2,1)}, u32[]{:S(2)}) copy-start(bf16[4,64,2,128]{3,2,1,0:T(2,128)(2,1)} %param.13) | copy-start | bytes 393220
  60.7 149.9 %all-reduce.7.cloned.1.call-start = ((), (), s32[]{:S(2)}) async-start(), calls=%async_computation.4 | async-start | bytes 4194304 | tf_op jit(solution)/shard_map/psum | solution.py:11
  121.1 117.5 %reduce-scatter.3.cloned.1.call-start = ((), (), s32[]{:S(2)}) async-start(), calls=%async_computation.5 | async-start | bytes 409600 | tf_op jit(solution)/shard_map/reduce_scatter | solution.py:59
  213.7 24.9 %copy-start.4 = (bf16[64,640]{1,0:T(8,128)(2,1)S(1)}, bf16[64,640]{1,0:T(8,128)(2,1)}, u32[]{:S(2)}) copy-start(bf16[64,640]{1,0:T(8,128)(2,1)} %param.16) | copy-start | bytes 245764
  218.9 114.6 %all-reduce.9.cloned.1.call-start = ((), (), s32[]{:S(2)}) async-start(), calls=%async_computation.6 | async-start | bytes 3145728 | tf_op jit(solution)/shard_map/psum | solution.py:66
  239.5 51.2 %copy-start.2 = (bf16[64,640]{1,0:T(8,128)(2,1)}, bf16[64,640]{1,0:T(8,128)(2,1)S(1)}, u32[]{:S(2)}) copy-start(bf16[64,640]{1,0:T(8,128)(2,1)S(1)} %add_convert_fusion) | copy-start | bytes 245764
  284.1 49.5 %copy-start.5 = (f32[3072]{0:T(1024)S(1)}, f32[3072]{0:T(1024)}, u32[]{:S(2)}) copy-start(f32[3072]{0:T(1024)} %param.19) | copy-start | bytes 36868
  290.7 117.1 %copy-start.6 = (f32[1280]{0:T(1024)S(1)}, f32[1280]{0:T(1024)}, u32[]{:S(2)}) copy-start(f32[1280]{0:T(1024)} %param.21) | copy-start | bytes 15364
  290.7 117.1 %reduce-scatter.5.cloned.1.call-start = ((), (), s32[]{:S(2)}) async-start(), calls=%async_computation.7 | async-start | bytes 1474560 | tf_op jit(solution)/shard_map/reduce_scatter | solution.py:69
  342.4 147.5 %all-reduce.11.cloned.1.call-start = ((), (), s32[]{:S(2)}) async-start(), calls=%async_computation.8 | async-start | bytes 3145728 | tf_op jit(solution)/shard_map/psum | solution.py:88
  440.8 0.8 copy-start.1
Sparse Core Ops, SparseCore 0:
  60.8 60.2 all-reduce.4
  123.4 87.1 all-reduce.6
  219.1 19.4 reduce-scatter.2
  290.8 42.7 all-reduce.8
  342.5 65.1 reduce-scatter.4
  448.4 41.4 all-reduce.10
